TPU v7x, 32 devices: a whole 2x2x4 slice. The times are simulated.
32 devices in a mesh: rows: 8 (over z, y), cols: 4 (over x, core).
Axes of the slice: x: 2, y: 2, z: 4, core: 2. Of those that a mesh axis runs over, the one named last changes fastest.
Arguments:
- points: bfloat16 [4096, 256], P(('rows', 'cols')), may hold values from -6 to 6
- start_vectors: float32 [8, 4096], P(None, ('rows', 'cols')), may hold values from -6 to 6
- degree: bfloat16 [4096], P(('rows', 'cols')), may hold values from 0.19921875 to 2
Outputs:
- embedding: float32 [8, 4096], P(None, ('rows', 'cols'))
All inputs are finite; a program needn't handle non-finite values.
Results may differ from a plain program's by a relative error of at most 0.0034.
Values may be sent and summed in bfloat16 or wider, within the bound.
A program may use at most 64 MiB of HBM per device.

v0:
```python
import jax
import jax.numpy as jnp
from jax import lax
from jax.sharding import PartitionSpec as P

ITERS = 3


def body(points, start_vectors, degree):
    row_count = lax.axis_size("rows")
    col_count = lax.axis_size("cols")
    row_place = lax.axis_index("rows")
    col_place = lax.axis_index("cols")
    span_size = points.shape[0]
    sharpness = 4.0 / points.shape[1]
    row_points, row_degree = (
        lax.all_gather(points, "cols", axis=0, tiled=True),
        lax.all_gather(degree, "cols", axis=0, tiled=True),
    )
    row_total = row_points.shape[0]
    row_float = row_points.astype(jnp.float32)
    row_norms = jnp.sum(row_float * row_float, axis=1)
    row_slots = jnp.arange(row_total, dtype=jnp.int32)
    row_global = (
        row_place * col_count + row_slots // span_size
    ) * span_size + row_slots % span_size

    def kernel_block(x_block, col_norms, first_slot):
        inner = lax.dot_general(
            row_points, x_block, (((1,), (1,)), ((), ())), preferred_element_type=jnp.float32
        )
        distance = row_norms[:, None] + col_norms[None, :] - 2.0 * inner
        kernel = jnp.exp(-sharpness * distance)
        col_slots = first_slot + jnp.arange(x_block.shape[0], dtype=jnp.int32)
        col_global = (
            col_slots // span_size * col_count + col_place
        ) * span_size + col_slots % span_size
        return jnp.where(
            row_global[:, None] == col_global[None, :], jnp.float32(0.0), kernel
        ).astype(jnp.bfloat16)

    vectors = start_vectors
    for iteration in range(ITERS):
        empty = jnp.zeros((vectors.shape[0], row_total), jnp.float32)
        sending = vectors.T.astype(jnp.bfloat16)
        x_piece = lax.all_gather(points, "rows", axis=0, tiled=True)
        v_piece = lax.all_gather(sending, "rows", axis=0, tiled=True)
        piece_rows = x_piece.shape[0]
        block_size = 512
        block_count = piece_rows // block_size

        def accumulate(block_index, running):
            offset = block_index * block_size
            x_block = lax.dynamic_slice_in_dim(x_piece, offset, block_size, 0)
            v_block = lax.dynamic_slice_in_dim(v_piece, offset, block_size, 0)
            x_float = x_block.astype(jnp.float32)
            col_norms = jnp.sum(x_float * x_float, axis=1)
            kernel = kernel_block(x_block, col_norms, offset)
            return running + lax.dot_general(
                v_block, kernel, (((0,), (1,)), ((), ())), preferred_element_type=jnp.float32
            )

        partial_value = lax.fori_loop(0, block_count, accumulate, empty)
        summed = lax.psum(partial_value, "cols")
        row_state = summed / row_degree.astype(jnp.float32)[None, :]
        vectors = lax.dynamic_slice_in_dim(row_state, col_place * span_size, span_size, 1)
    magnitude = lax.psum(jnp.sum(jnp.abs(row_state), axis=1), "rows")
    mean_abs = magnitude / (span_size * row_count * col_count)
    return vectors / (mean_abs[:, None] + 1e-06)


def solution(mesh):
    return jax.shard_map(
        body,
        mesh=mesh,
        in_specs=(P(("rows", "cols"), None), P(None, ("rows", "cols")), P(("rows", "cols"))),
        out_specs=P(None, ("rows", "cols")),
        check_vma=False,
    )
```

profile of v0, /device:TPU:0, one launch (start us, length us, event | category | flops | bytes accessed | tf_op | source)
XLA Modules:
  0.0 177.6 jit_solution(2372064318550203494)
XLA Ops:
  0.0 0.7 copy-done.2
  0.7 6.0 %all-gather = bf16[4,1,128]{2,1,0:T(2,128)(2,1)S(1)} all-gather(bf16[1,1,128]{2,1,0:T(2,128)(2,1)S(1)} %bitcast.73), channel_id=1, replica_groups=mesh['rows'=8,'cols'=4] {'cols'}, dimensions={0}, use_global_device_ids=true | all-gather | bytes 1280 | tf_op jit(solution)/shard_map/all_gather | solution.py:18
  6.7 6.5 %all_gather.21 = bf16[512,256]{1,0:T(8,128)(2,1)S(1)} all-gather(bf16[128,256]{1,0:T(8,128)(2,1)} %param.9), channel_id=1, replica_groups=mesh['rows'=8,'cols'=4] {'cols'}, dimensions={0}, use_global_device_ids=true | all-gather | bytes 327680 | tf_op jit(solution)/shard_map/all_gather | solution.py:17
  13.4 0.7 copy-done
  14.0 32.1 %all_gather.22 = bf16[1024,256]{1,0:T(8,128)(2,1)S(1)} all-gather(bf16[128,256]{1,0:T(8,128)(2,1)S(1)} %copy-done), channel_id=1, replica_groups=mesh['rows'=8,'cols'=4] {'rows'}, dimensions={0}, use_global_device_ids=true | all-gather | bytes 589824 | tf_op jit(solution)/shard_map/all_gather | solution.py:46
  46.2 26.1 %all_gather.20 = bf16[1024,8]{0,1:T(8,128)(2,1)S(1)} all-gather(bf16[128,8]{0,1:T(8,128)(2,1)S(1)} %convert_bitcast_fusion), channel_id=1, replica_groups=mesh['rows'=8,'cols'=4] {'rows'}, dimensions={0}, use_global_device_ids=true | all-gather | bytes 18432 | tf_op jit(solution)/shard_map/all_gather | solution.py:47
  72.3 1.6 while.48
  72.5 0.6 fusion.155
  73.1 0.2 multiply_reduce_fusion.7
  73.3 0.6 fusion.155
  73.9 10.1 %psum.28 = f32[8,512]{1,0:T(8,128)S(1)} all-reduce(f32[8,512]{1,0:T(8,128)S(1)} %get-tuple-element.608), channel_id=1, replica_groups=mesh['rows'=8,'cols'=4] {'cols'}, use_global_device_ids=true, to_apply=%region_4.5 | all-reduce | flops 4096 | bytes 32768 | tf_op jit(solution)/shard_map/psum | solution.py:64
  84.0 26.1 %all_gather.24 = bf16[1024,8]{0,1:T(8,128)(2,1)S(1)} all-gather(bf16[128,8]{0,1:T(8,128)(2,1)S(1)} %fusion.131), channel_id=1, replica_groups=mesh['rows'=8,'cols'=4] {'rows'}, dimensions={0}, use_global_device_ids=true | all-gather | bytes 18432 | tf_op jit(solution)/shard_map/all_gather | solution.py:47
  110.1 1.6 while.49
  110.3 0.6 fusion.160
  110.9 0.2 multiply_reduce_fusion.8
  111.1 0.6 fusion.160
  111.7 10.1 %psum.29 = f32[8,512]{1,0:T(8,128)S(1)} all-reduce(f32[8,512]{1,0:T(8,128)S(1)} %get-tuple-element.609), channel_id=1, replica_groups=mesh['rows'=8,'cols'=4] {'cols'}, use_global_device_ids=true, to_apply=%region_8.9 | all-reduce | flops 4096 | bytes 32768 | tf_op jit(solution)/shard_map/psum | solution.py:64
  121.8 26.1 %all_gather.25 = bf16[1024,8]{0,1:T(8,128)(2,1)S(1)} all-gather(bf16[128,8]{0,1:T(8,128)(2,1)S(1)} %fusion.132), channel_id=1, replica_groups=mesh['rows'=8,'cols'=4] {'rows'}, dimensions={0}, use_global_device_ids=true | all-gather | bytes 18432 | tf_op jit(solution)/shard_map/all_gather | solution.py:47
  148.0 1.6 while.50
  148.1 0.6 fusion.165
  148.9 0.6 fusion.165
  149.5 10.1 %psum.30 = f32[8,512]{1,0:T(8,128)S(1)} all-reduce(f32[8,512]{1,0:T(8,128)S(1)} %get-tuple-element.610), channel_id=1, replica_groups=mesh['rows'=8,'cols'=4] {'cols'}, use_global_device_ids=true, to_apply=%region_12.13 | all-reduce | flops 4096 | bytes 32768 | tf_op jit(solution)/shard_map/psum | solution.py:64
  159.8 17.1 %psum.31 = f32[8]{0:T(128)S(1)} all-reduce(f32[8]{0:T(128)S(1)} %get-tuple-element.749), channel_id=1, replica_groups=mesh['rows'=8,'cols'=4] {'rows'}, use_global_device_ids=true, to_apply=%region_14.15 | all-reduce | flops 8 | bytes 64 | tf_op jit(solution)/shard_map/psum | solution.py:67
  176.9 0.7 dynamic-slice_divide_fusion.2
  (25 shorter events, 1.1 us)
Async XLA Ops:
  0.0 0.7 copy-start.2
  13.2 0.8 copy-start
  14.0 32.1 %copy-start.1 = (f32[8,128]{1,0:T(8,128)S(1)}, f32[8,128]{1,0:T(8,128)}, u32[]{:S(2)}) copy-start(f32[8,128]{1,0:T(8,128)} %param.10) | copy-start | bytes 12292
where the time goes:
time: 178 us
  blocking collectives  170 us (96%)
  matrix products  3.57 us (2%)
  other arithmetic  2.03 us (1%)
    all_gather x3, blocking collectives, body(): v_piece = lax.all_gather(sending, 'rows', axis=0, tiled=True)  78.3 us
    all_gather x1, blocking collectives, body(): x_piece = lax.all_gather(points, 'rows', axis=0, tiled=True)  32.1 us
    psum x3, blocking collectives, body(): summed = lax.psum(partial_value, 'cols')  30.4 us
    psum x1, blocking collectives, body(): magnitude = lax.psum(jnp.sum(jnp.abs(row_state), axis=1), 'rows')  17.1 us
    all_gather x1, blocking collectives, body(): lax.all_gather(points, 'cols', axis=0, tiled=True)  6.47 us
    all_gather x1, blocking collectives, body(): lax.all_gather(degree, 'cols', axis=0, tiled=True)  5.99 us
    dot_general x6, matrix products, accumulate(): lax.dot_general(v_block, kernel, (((0,), (1,)), ((), ())), preferred_elem...  3.57 us

commit v1 on v0

--- a/solution.py
+++ b/solution.py
@@ -43,7 +43,23 @@
     for iteration in range(ITERS):
         empty = jnp.zeros((vectors.shape[0], row_total), jnp.float32)
         sending = vectors.T.astype(jnp.bfloat16)
-        x_piece = lax.all_gather(points, "rows", axis=0, tiled=True)
+        size, mine, rows = (lax.axis_size("rows"), lax.axis_index("rows"), points.shape[0])
+        ahead = [(i, (i + 1) % size) for i in range(size)]
+        backward = [(i, (i - 1) % size) for i in range(size)]
+        x_piece = jnp.zeros((*points.shape[:0], size * rows, *points.shape[0 + 1 :]), points.dtype)
+        x_piece = lax.dynamic_update_slice_in_dim(x_piece, points, mine * rows, axis=0)
+        from_left = from_right = points
+        half = size // 2
+        for step in range(1, half + 1):
+            from_left = lax.ppermute(from_left, "rows", ahead)
+            x_piece = lax.dynamic_update_slice_in_dim(
+                x_piece, from_left, (mine - step) % size * rows, axis=0
+            )
+            if step < size - half:
+                from_right = lax.ppermute(from_right, "rows", backward)
+                x_piece = lax.dynamic_update_slice_in_dim(
+                    x_piece, from_right, (mine + step) % size * rows, axis=0
+                )
         v_piece = lax.all_gather(sending, "rows", axis=0, tiled=True)
         piece_rows = x_piece.shape[0]
         block_size = 512

time: 178 us -> 172 us (0.966)
  blocking collectives: 170 us -> 137 us
  starting transfers between devices: 0 us -> 15.5 us
  waiting for transfers between devices: 0 us -> 11.4 us
    all_gather x1 -> x0, blocking collectives: 32.1 us -> none  [body(): x_piece = lax.all_gather(points, 'rows', axis=0, tiled=True)]
    ppermute x0 -> x7, starting transfers between devices: none -> 15.5 us  [the longest x3 12.5 us: body(): from_right = lax.ppermute(from_right, 'rows', backward)]
    ppermute x0 -> x7, waiting for transfers between devices: none -> 11.4 us  [the longest x4 11.4 us: body(): from_left = lax.ppermute(from_left, 'rows', ahead)]
  transfers between devices with their start and end apart: 0 -> 7, of which waited for: 0 -> 3; matrix products, arithmetic and copies ran while one was open for 0% -> 0% of each run, Pallas kernels for 0% -> 0%
where the time goes in v1:
time: 172 us
  blocking collectives  137 us (80%)
  starting transfers between devices  15.5 us (9%)
  waiting for transfers between devices  11.4 us (7%)
  matrix products  3.57 us (2%)
  local copies, waits for them, and re-layouts  2.26 us (1%)
  other arithmetic  2.04 us (1%)
    all_gather x3, blocking collectives, body(): v_piece = lax.all_gather(sending, 'rows', axis=0, tiled=True)  78.3 us
    psum x3, blocking collectives, body(): summed = lax.psum(partial_value, 'cols')  30.4 us
    psum x1, blocking collectives, body(): magnitude = lax.psum(jnp.sum(jnp.abs(row_state), axis=1), 'rows')  17.1 us
    ppermute x3, starting transfers between devices, body(): from_right = lax.ppermute(from_right, 'rows', backward)  12.5 us
    ppermute x4, waiting for transfers between devices, body(): from_left = lax.ppermute(from_left, 'rows', ahead)  11.4 us
    all_gather x1, blocking collectives, body(): lax.all_gather(points, 'cols', axis=0, tiled=True)  5.89 us
    all_gather x1, blocking collectives, body(): lax.all_gather(degree, 'cols', axis=0, tiled=True)  5.05 us
    dot_general x6, matrix products, accumulate(): lax.dot_general(v_block, kernel, (((0,), (1,)), ((), ())), preferred_elem...  3.57 us
  transfers between devices with their start and end apart: 7, of which 3 were waited for; matrix products, arithmetic and copies ran while one was open for 0% of the time, Pallas kernels for 0%

profile of v1, /device:TPU:0, one launch (start us, length us, event | category | flops | bytes accessed | tf_op | source)
XLA Modules:
  0.0 171.8 jit_solution(5542084124059363002)
XLA Ops:
  0.0 3.0 %collective-permute-start = (bf16[128,256]{1,0:T(8,128)(2,1)}, bf16[128,256]{1,0:T(8,128)(2,1)S(1)}, u32[]{:S(2)}, u32[]{:S(2)}) collective-permute-start(bf16[128,256]{1,0:T(8,128)(2,1)} %param.9), channel_id=1, source_target_pairs={{0,4},{4,8},{8,12},{12,16},{16,20},{20,24},{24,28},{28,0},{1,5},{5... | collective-permute-start | bytes 196616 | tf_op jit(solution)/shard_map/ppermute | solution.py:54
  3.0 3.0 %collective-permute-start.1 = (bf16[128,256]{1,0:T(8,128)(2,1)}, bf16[128,256]{1,0:T(8,128)(2,1)S(1)}, u32[]{:S(2)}, u32[]{:S(2)}) collective-permute-start(bf16[128,256]{1,0:T(8,128)(2,1)} %param.9), channel_id=1, source_target_pairs={{0,28},{4,0},{8,4},{12,8},{16,12},{20,16},{24,20},{28,24},{1,29},{... | collective-permute-start | bytes 196616 | tf_op jit(solution)/shard_map/ppermute | solution.py:59
  6.0 0.9 copy-done
  6.9 5.9 %all_gather.16 = bf16[512,256]{1,0:T(8,128)(2,1)S(1)} all-gather(bf16[128,256]{1,0:T(8,128)(2,1)S(1)} %copy-done), channel_id=1, replica_groups=mesh['rows'=8,'cols'=4] {'cols'}, dimensions={0}, use_global_device_ids=true | all-gather | bytes 327680 | tf_op jit(solution)/shard_map/all_gather | solution.py:17
  13.5 26.1 %all_gather.15 = bf16[1024,8]{0,1:T(8,128)(2,1)S(1)} all-gather(bf16[128,8]{0,1:T(8,128)(2,1)S(1)} %convert_bitcast_fusion), channel_id=1, replica_groups=mesh['rows'=8,'cols'=4] {'rows'}, dimensions={0}, use_global_device_ids=true | all-gather | bytes 18432 | tf_op jit(solution)/shard_map/all_gather | solution.py:63
  39.6 0.7 copy-done.2
  40.3 5.0 %all-gather = bf16[4,1,128]{2,1,0:T(2,128)(2,1)S(1)} all-gather(bf16[1,1,128]{2,1,0:T(2,128)(2,1)S(1)} %bitcast.73), channel_id=1, replica_groups=mesh['rows'=8,'cols'=4] {'cols'}, dimensions={0}, use_global_device_ids=true | all-gather | bytes 1280 | tf_op jit(solution)/shard_map/all_gather | solution.py:18
  45.5 4.7 %collective-permute-start.3 = (bf16[128,256]{1,0:T(8,128)(2,1)S(1)}, bf16[128,256]{1,0:T(8,128)(2,1)S(1)}, u32[]{:S(2)}, u32[]{:S(2)}) collective-permute-start(bf16[128,256]{1,0:T(8,128)(2,1)S(1)} %collective-permute-done.1), channel_id=1, source_target_pairs={{0,28},{4,0},{8,4},{12,8},{16,12},{20,16},{24,20},{28,24},{1,29},{... | collective-permute-start | bytes 196616 | tf_op jit(solution)/shard_map/ppermute | solution.py:59
  50.3 2.3 %collective-permute-done.2 = bf16[128,256]{1,0:T(8,128)(2,1)S(1)} collective-permute-done((bf16[128,256]{1,0:T(8,128)(2,1)S(1)}, bf16[128,256]{1,0:T(8,128)(2,1)S(1)}, u32[]{:S(2)}, u32[]{:S(2)}) %collective-permute-start.2) | collective-permute-done | bytes 65568 | tf_op jit(solution)/shard_map/ppermute | solution.py:54
  52.6 4.7 %collective-permute-start.5 = (bf16[128,256]{1,0:T(8,128)(2,1)S(1)}, bf16[128,256]{1,0:T(8,128)(2,1)S(1)}, u32[]{:S(2)}, u32[]{:S(2)}) collective-permute-start(bf16[128,256]{1,0:T(8,128)(2,1)S(1)} %collective-permute-done.3), channel_id=1, source_target_pairs={{0,28},{4,0},{8,4},{12,8},{16,12},{20,16},{24,20},{28,24},{1,29},{... | collective-permute-start | bytes 196616 | tf_op jit(solution)/shard_map/ppermute | solution.py:59
  57.3 2.2 %collective-permute-done.4 = bf16[128,256]{1,0:T(8,128)(2,1)S(1)} collective-permute-done((bf16[128,256]{1,0:T(8,128)(2,1)S(1)}, bf16[128,256]{1,0:T(8,128)(2,1)S(1)}, u32[]{:S(2)}, u32[]{:S(2)}) %collective-permute-start.4) | collective-permute-done | bytes 65568 | tf_op jit(solution)/shard_map/ppermute | solution.py:54
  59.6 6.9 %collective-permute-done.6 = bf16[128,256]{1,0:T(8,128)(2,1)S(1)} collective-permute-done((bf16[128,256]{1,0:T(8,128)(2,1)S(1)}, bf16[128,256]{1,0:T(8,128)(2,1)S(1)}, u32[]{:S(2)}, u32[]{:S(2)}) %collective-permute-start.6) | collective-permute-done | bytes 65568 | tf_op jit(solution)/shard_map/ppermute | solution.py:54
  66.5 1.6 while.48
  68.1 10.1 %psum.28 = f32[8,512]{1,0:T(8,128)S(1)} all-reduce(f32[8,512]{1,0:T(8,128)S(1)} %get-tuple-element.608), channel_id=1, replica_groups=mesh['rows'=8,'cols'=4] {'cols'}, use_global_device_ids=true, to_apply=%region_4.5 | all-reduce | flops 4096 | bytes 32768 | tf_op jit(solution)/shard_map/psum | solution.py:80
  78.2 26.1 %all_gather.18 = bf16[1024,8]{0,1:T(8,128)(2,1)S(1)} all-gather(bf16[128,8]{0,1:T(8,128)(2,1)S(1)} %fusion.131), channel_id=1, replica_groups=mesh['rows'=8,'cols'=4] {'rows'}, dimensions={0}, use_global_device_ids=true | all-gather | bytes 18432 | tf_op jit(solution)/shard_map/all_gather | solution.py:63
  104.3 1.6 while.49
  105.9 10.1 %psum.29 = f32[8,512]{1,0:T(8,128)S(1)} all-reduce(f32[8,512]{1,0:T(8,128)S(1)} %get-tuple-element.609), channel_id=1, replica_groups=mesh['rows'=8,'cols'=4] {'cols'}, use_global_device_ids=true, to_apply=%region_8.9 | all-reduce | flops 4096 | bytes 32768 | tf_op jit(solution)/shard_map/psum | solution.py:80
  116.0 26.1 %all_gather.19 = bf16[1024,8]{0,1:T(8,128)(2,1)S(1)} all-gather(bf16[128,8]{0,1:T(8,128)(2,1)S(1)} %fusion.132), channel_id=1, replica_groups=mesh['rows'=8,'cols'=4] {'rows'}, dimensions={0}, use_global_device_ids=true | all-gather | bytes 18432 | tf_op jit(solution)/shard_map/all_gather | solution.py:63
  142.2 1.6 while.50
  142.3 0.6 fusion.165
  143.1 0.6 fusion.165
  143.7 10.1 %psum.30 = f32[8,512]{1,0:T(8,128)S(1)} all-reduce(f32[8,512]{1,0:T(8,128)S(1)} %get-tuple-element.610), channel_id=1, replica_groups=mesh['rows'=8,'cols'=4] {'cols'}, use_global_device_ids=true, to_apply=%region_12.13 | all-reduce | flops 4096 | bytes 32768 | tf_op jit(solution)/shard_map/psum | solution.py:80
  154.0 17.1 %psum.31 = f32[8]{0:T(128)S(1)} all-reduce(f32[8]{0:T(128)S(1)} %get-tuple-element.749), channel_id=1, replica_groups=mesh['rows'=8,'cols'=4] {'rows'}, use_global_device_ids=true, to_apply=%region_14.15 | all-reduce | flops 8 | bytes 64 | tf_op jit(solution)/shard_map/psum | solution.py:83
  171.1 0.7 dynamic-slice_divide_fusion.2
  (47 shorter events, 4.5 us)
Async XLA Ops:
  0.0 45.5 %collective-permute-start = (bf16[128,256]{1,0:T(8,128)(2,1)}, bf16[128,256]{1,0:T(8,128)(2,1)S(1)}, u32[]{:S(2)}, u32[]{:S(2)}) collective-permute-start(bf16[128,256]{1,0:T(8,128)(2,1)} %param.9), channel_id=1, source_target_pairs={{0,4},{4,8},{8,12},{12,16},{16,20},{20,24},{24,28},{28,0},{1,5},{5... | collective-permute-start | bytes 196616 | tf_op jit(solution)/shard_map/ppermute | solution.py:54
  3.0 42.5 %collective-permute-start.1 = (bf16[128,256]{1,0:T(8,128)(2,1)}, bf16[128,256]{1,0:T(8,128)(2,1)S(1)}, u32[]{:S(2)}, u32[]{:S(2)}) collective-permute-start(bf16[128,256]{1,0:T(8,128)(2,1)} %param.9), channel_id=1, source_target_pairs={{0,28},{4,0},{8,4},{12,8},{16,12},{20,16},{24,20},{28,24},{1,29},{... | collective-permute-start | bytes 196616 | tf_op jit(solution)/shard_map/ppermute | solution.py:59
  6.0 0.9 copy-start
  12.8 0.7 copy-start.1
  39.6 0.7 copy-start.2
  45.5 7.1 %collective-permute-start.2 = (bf16[128,256]{1,0:T(8,128)(2,1)S(1)}, bf16[128,256]{1,0:T(8,128)(2,1)S(1)}, u32[]{:S(2)}, u32[]{:S(2)}) collective-permute-start(bf16[128,256]{1,0:T(8,128)(2,1)S(1)} %collective-permute-done), channel_id=1, source_target_pairs={{0,4},{4,8},{8,12},{12,16},{16,20},{20,24},{24,28},{28,0},{1,5},{5... | collective-permute-start | bytes 196616 | tf_op jit(solution)/shard_map/ppermute | solution.py:54
  45.5 7.0 %collective-permute-start.3 = (bf16[128,256]{1,0:T(8,128)(2,1)S(1)}, bf16[128,256]{1,0:T(8,128)(2,1)S(1)}, u32[]{:S(2)}, u32[]{:S(2)}) collective-permute-start(bf16[128,256]{1,0:T(8,128)(2,1)S(1)} %collective-permute-done.1), channel_id=1, source_target_pairs={{0,28},{4,0},{8,4},{12,8},{16,12},{20,16},{24,20},{28,24},{1,29},{... | collective-permute-start | bytes 196616 | tf_op jit(solution)/shard_map/ppermute | solution.py:59
  52.6 7.0 %collective-permute-start.4 = (bf16[128,256]{1,0:T(8,128)(2,1)S(1)}, bf16[128,256]{1,0:T(8,128)(2,1)S(1)}, u32[]{:S(2)}, u32[]{:S(2)}) collective-permute-start(bf16[128,256]{1,0:T(8,128)(2,1)S(1)} %collective-permute-done.2), channel_id=1, source_target_pairs={{0,4},{4,8},{8,12},{12,16},{16,20},{20,24},{24,28},{28,0},{1,5},{5... | collective-permute-start | bytes 196616 | tf_op jit(solution)/shard_map/ppermute | solution.py:54
  52.6 7.0 %collective-permute-start.5 = (bf16[128,256]{1,0:T(8,128)(2,1)S(1)}, bf16[128,256]{1,0:T(8,128)(2,1)S(1)}, u32[]{:S(2)}, u32[]{:S(2)}) collective-permute-start(bf16[128,256]{1,0:T(8,128)(2,1)S(1)} %collective-permute-done.3), channel_id=1, source_target_pairs={{0,28},{4,0},{8,4},{12,8},{16,12},{20,16},{24,20},{28,24},{1,29},{... | collective-permute-start | bytes 196616 | tf_op jit(solution)/shard_map/ppermute | solution.py:59
  59.5 7.0 %collective-permute-start.6 = (bf16[128,256]{1,0:T(8,128)(2,1)S(1)}, bf16[128,256]{1,0:T(8,128)(2,1)S(1)}, u32[]{:S(2)}, u32[]{:S(2)}) collective-permute-start(bf16[128,256]{1,0:T(8,128)(2,1)S(1)} %collective-permute-done.4), channel_id=1, source_target_pairs={{0,4},{4,8},{8,12},{12,16},{16,20},{20,24},{24,28},{28,0},{1,5},{5... | collective-permute-start | bytes 196616 | tf_op jit(solution)/shard_map/ppermute | solution.py:54
